TPU v7x, 256 devices: a whole 4x4x8 slice. The times are simulated.
256 devices in a mesh: rows: 64 (over z, y, core), cols: 4 (over x).
Axes of the slice: x: 4, y: 4, z: 8, core: 2. Of those that a mesh axis runs over, the one named last changes fastest.
Arguments:
- gradients: float32 [256, 128, 4096], P(None, 'rows', 'cols'), may hold values from -6 to 6
- momentum: float32 [256, 128, 4096], P(None, 'rows', 'cols'), may hold values from -6 to 6
- weights: float32 [256, 128, 4096], P(None, 'rows', 'cols'), may hold values from -0.1875 to 0.1875
Outputs:
- new_weights: float32 [256, 128, 4096], P(None, 'rows', 'cols')
- new_momentum: float32 [256, 128, 4096], P(None, 'rows', 'cols')
All inputs are finite; a program needn't handle non-finite values.
Results may differ from a plain program's by a relative error of at most 0.0003.
Values sent between devices are 32-bit elements.
A program may use at most 64 MiB of HBM per device.

v0:
```python
import jax
import jax.numpy as jnp
from jax import lax
from jax.sharding import PartitionSpec as P

ITERS = 4
hold_rate = 0.8
learn_rate = 0.8
decay_rate = 0.1


def local(gradients, momentum, weights):
    new_momentum = hold_rate * momentum + gradients
    moved = lax.all_to_all(new_momentum, "rows", split_axis=0, concat_axis=1, tiled=True)
    whole = lax.all_to_all(moved, "cols", split_axis=0, concat_axis=2, tiled=True)
    iterate = whole * lax.rsqrt(jnp.sum(whole * whole, axis=(1, 2), keepdims=True) + 1e-06)
    for step in range(ITERS):
        gram = jnp.einsum("mik,mjk->mij", iterate, iterate, precision=lax.Precision.HIGHEST)
        mixed = -4.775 * gram + 2.0315 * jnp.einsum(
            "mij,mjk->mik", gram, gram, precision=lax.Precision.HIGHEST
        )
        iterate = 3.4445 * iterate + jnp.einsum(
            "mij,mjk->mik", mixed, iterate, precision=lax.Precision.HIGHEST
        )
    iterate = lax.all_to_all(iterate, "cols", split_axis=2, concat_axis=0, tiled=True)
    back = lax.all_to_all(iterate, "rows", split_axis=1, concat_axis=0, tiled=True)
    new_weights = (1.0 - learn_rate * decay_rate) * weights - learn_rate * back
    return (new_weights, new_momentum)


def solution(mesh):
    placed = (P(None, "rows", "cols"), P(None, "rows", "cols"), P(None, "rows", "cols"))
    return jax.shard_map(
        local,
        mesh=mesh,
        in_specs=placed,
        out_specs=(P(None, "rows", "cols"), P(None, "rows", "cols")),
        check_vma=False,
    )
```

profile of v0, /device:TPU:8, one launch (start us, length us, event | category | flops | bytes accessed | tf_op | source)
XLA Modules:
  0.0 229.1 jit_solution(2761105436010172675)
XLA Ops:
  0.6 3.7 %multiply_add_fusion = f32[256,2,1024]{2,1,0:T(2,128)S(1)} fusion(f32[256,2,1024]{2,1,0:T(2,128)} %param.3, f32[256,2,1024]{2,1,0:T(2,128)} %param.4), kind=kLoop, calls=%fused_computation.11 | loop fusion | flops 1048576 | bytes 6291456 | tf_op jit(solution)/shard_map/add | solution.py:13
  4.3 0.0 copy-start
  4.3 63.1 %all_to_all.54 = f32[256,2,1024]{2,1,0:T(2,128)S(1)} all-to-all(f32[256,2,1024]{2,1,0:T(2,128)S(1)} %multiply_add_fusion), channel_id=1, replica_groups=mesh['rows'=64,'cols'=4] {'rows'}, dimensions={0} | all-to-all | bytes 4194304 | tf_op jit(solution)/shard_map/all_to_all | solution.py:14
  67.4 0.0 copy-done
  67.4 0.8 copy.32
  68.3 2.4 %all_to_all.43 = f32[4,128,1024]{2,1,0:T(8,128)} reshape(f32[4,64,2,1024]{3,2,1,0:T(2,128)S(1)} %bitcast.56) | data formatting | bytes 4194304 | tf_op jit(solution)/shard_map/all_to_all | solution.py:14
  70.7 29.1 %all_to_all.55 = f32[4,128,1024]{2,1,0:T(8,128)S(1)} all-to-all(f32[4,128,1024]{2,1,0:T(8,128)} %all_to_all.43), channel_id=1, replica_groups=mesh['rows'=64,'cols'=4] {'cols'}, dimensions={0} | all-to-all | bytes 4194304 | tf_op jit(solution)/shard_map/all_to_all | solution.py:15
  99.8 1.1 multiply_reduce_fusion
  101.6 1.8 fusion.4
  103.4 0.2 fusion.10
  103.6 2.6 %multiply_bitcast_fusion.1 = (f32[1,128,4,1024]{3,1,2,0:T(8,128)}, f32[1,128,4,1024]{3,1,2,0:T(8,128)}) fusion(f32[4,128,1024]{2,1,0:T(8,128)S(1)} %all_to_all.55, f32[]{:T(128)S(6)} %rsqrt.4), kind=kLoop, calls=%fused_computation.13 | loop fusion | flops 1048576 | bytes 6291460 | tf_op jit(solution)/shard_map/mul | solution.py:16
  106.2 1.9 copy.26
  108.1 2.9 %copy.25 = f32[1,128,4,1024]{1,3,2,0:T(8,128)} copy(f32[1,128,4,1024]{3,1,2,0:T(8,128)} %get-tuple-element.3) | data formatting | bytes 4194304 | tf_op jit(solution)/shard_map/mul | solution.py:22
  111.0 3.0 %copy.27 = f32[128,4096]{1,0:T(8,128)} copy(f32[128,4096]{0,1:T(8,128)} %bitcast.57) | data formatting | bytes 4194304 | tf_op jit(solution)/shard_map/mul | solution.py:22
  114.0 3.6 %convolution_add_fusion.3 = f32[128,4096]{1,0:T(8,128)S(1)} fusion(f32[128,4096]{1,0:T(8,128)} %copy.27, f32[128,128]{1,0:T(8,128)S(1)} %fusion.10, f32[128,4096]{0,1:T(8,128)S(1)} %bitcast.55), kind=kOutput, calls=%fused_computation.4 | convolution fusion | flops 805830656 | bytes 6356992 | tf_op jit(solution)/shard_map/mij,mjk->mik/dot_general | solution.py:22
  117.5 1.8 fusion.12
  119.3 0.2 fusion.9
  119.6 2.0 convolution_add_fusion.2
  121.6 1.8 fusion.13
  123.4 0.2 fusion.8
  123.6 2.0 convolution_add_fusion.1
  125.7 1.8 fusion.14
  127.5 0.2 fusion.7
  127.7 2.3 fusion
  130.0 3.7 %copy.28 = f32[1,128,4096]{1,0,2:T(1,128)} copy(f32[1,128,4096]{2,1,0:T(8,128)S(1)} %fusion) | data formatting | bytes 4194304 | tf_op jit(solution)/shard_map/add | solution.py:22
  133.7 27.5 %all_to_all.56 = f32[1,128,4096]{1,0,2:T(1,128)S(1)} all-to-all(f32[1,128,4096]{1,0,2:T(1,128)} %copy.28), channel_id=1, replica_groups=mesh['rows'=64,'cols'=4] {'cols'}, dimensions={2} | all-to-all | bytes 4194304 | tf_op jit(solution)/shard_map/all_to_all | solution.py:25
  161.2 2.0 copy.29
  163.1 60.5 %all_to_all.57 = f32[4,128,1024]{2,0,1:T(4,128)S(1)} all-to-all(f32[4,128,1024]{2,0,1:T(4,128)} %bitcast.59), channel_id=1, replica_groups=mesh['rows'=64,'cols'=4] {'rows'}, dimensions={1} | all-to-all | bytes 4194304 | tf_op jit(solution)/shard_map/all_to_all | solution.py:26
  223.7 0.6 broadcast_multiply_fusion
  224.2 0.0 copy-start.1
  224.3 1.9 copy.30
  226.2 0.0 copy-done.1
  226.2 2.9 %bitcast_subtract_fusion = f32[256,2,1024]{2,1,0:T(2,128)} fusion(f32[64,4,2,1024]{3,2,1,0:T(2,128)S(1)} %copy.30, f32[256,2,1024]{2,1,0:T(2,128)S(1)} %copy-done.1), kind=kLoop, calls=%fused_computation.7 | loop fusion | flops 1048576 | bytes 6291456 | tf_op jit(solution)/shard_map/sub | solution.py:27
Async XLA Ops:
  4.3 63.2 %copy-start = (f32[256,2,1024]{2,1,0:T(2,128)}, f32[256,2,1024]{2,1,0:T(2,128)S(1)}, u32[]{:S(2)}) copy-start(f32[256,2,1024]{2,1,0:T(2,128)S(1)} %multiply_add_fusion) | copy-start | bytes 6291460
  224.2 2.0 copy-start.1
where the time goes:
time: 230 us; the launch traced here: 229 us
  blocking collectives  180 us (78%)
  local copies, waits for them, and re-layouts  18.6 us (8%)
  matrix products  17.9 us (8%)
  other arithmetic  10.8 us (5%)
    all_to_all x1, blocking collectives, local(): lax.all_to_all(new_momentum, 'rows', split_axis=0, concat_axis=1, tiled=T...  63.1 us
    all_to_all x1, blocking collectives, local(): lax.all_to_all(iterate, 'rows', split_axis=1, concat_axis=0, tiled=True)  60.5 us
    all_to_all x1, blocking collectives, local(): lax.all_to_all(moved, 'cols', split_axis=0, concat_axis=2, tiled=True)  29.1 us
    all_to_all x1, blocking collectives, local(): lax.all_to_all(iterate, 'cols', split_axis=2, concat_axis=0, tiled=True)  27.5 us
    dot_general x4, matrix products, local(): jnp.einsum('mij,mjk->mik', mixed, iterate, precision=lax.Precision.HIGHEST)  9.94 us
    dot_general x4, matrix products, local(): jnp.einsum('mik,mjk->mij', iterate, iterate, precision=lax.Precision.HIGH...  7.17 us
    mul x2, local copies, waits for them, and re-layouts, local(): 3.4445 * iterate  5.84 us

commit v1 on v0

--- a/solution.py
+++ b/solution.py
@@ -22,7 +22,10 @@
         iterate = 3.4445 * iterate + jnp.einsum(
             "mij,mjk->mik", mixed, iterate, precision=lax.Precision.HIGHEST
         )
-    iterate = lax.all_to_all(iterate, "cols", split_axis=2, concat_axis=0, tiled=True)
+    iterate = jnp.concatenate(
+        lax.all_to_all(jnp.stack(jnp.split(iterate, lax.axis_size("cols"), axis=2)), "cols", 0, 0),
+        axis=0,
+    )
     back = lax.all_to_all(iterate, "rows", split_axis=1, concat_axis=0, tiled=True)
     new_weights = (1.0 - learn_rate * decay_rate) * weights - learn_rate * back
     return (new_weights, new_momentum)

time: 230 us -> 224 us (0.974)
  local copies, waits for them, and re-layouts: 18.6 us -> 14.5 us
    add x1 -> x0, local copies, waits for them, and re-layouts: 3.7 us -> none  [local(): 3.4445 * iterate]
where the time goes in v1:
time: 224 us
  blocking collectives  179 us (80%)
  matrix products  17.9 us (8%)
  local copies, waits for them, and re-layouts  14.5 us (6%)
  other arithmetic  11.1 us (5%)
    all_to_all x1, blocking collectives, local(): lax.all_to_all(new_momentum, 'rows', split_axis=0, concat_axis=1, tiled=T...  63.1 us
    all_to_all x1, blocking collectives, local(): lax.all_to_all(iterate, 'rows', split_axis=1, concat_axis=0, tiled=True)  60.3 us
    all_to_all x1, blocking collectives, local(): lax.all_to_all(moved, 'cols', split_axis=0, concat_axis=2, tiled=True)  29.1 us
    all_to_all x1, blocking collectives, local(): lax.all_to_all(jnp.stack(jnp.split(iterate, lax.axis_size('cols'), axis=2...  26.4 us
    dot_general x4, matrix products, local(): jnp.einsum('mij,mjk->mik', mixed, iterate, precision=lax.Precision.HIGHEST)  9.95 us
    dot_general x4, matrix products, local(): jnp.einsum('mik,mjk->mij', iterate, iterate, precision=lax.Precision.HIGH...  7.17 us
    mul x2, local copies, waits for them, and re-layouts, local(): 3.4445 * iterate  5.8 us

profile of v1, /device:TPU:8, one launch (start us, length us, event | category | flops | bytes accessed | tf_op | source)
XLA Modules:
  0.0 224.0 jit_solution(7043752736201725749)
XLA Ops:
  0.6 3.7 %multiply_add_fusion = f32[256,2,1024]{2,1,0:T(2,128)S(1)} fusion(f32[256,2,1024]{2,1,0:T(2,128)} %param.3, f32[256,2,1024]{2,1,0:T(2,128)} %param.4), kind=kLoop, calls=%fused_computation.12 | loop fusion | flops 1048576 | bytes 6291456 | tf_op jit(solution)/shard_map/add | solution.py:13
  4.3 0.0 copy-start
  4.3 63.1 %all_to_all.41 = f32[256,2,1024]{2,1,0:T(2,128)S(1)} all-to-all(f32[256,2,1024]{2,1,0:T(2,128)S(1)} %multiply_add_fusion), channel_id=1, replica_groups=mesh['rows'=64,'cols'=4] {'rows'}, dimensions={0} | all-to-all | bytes 4194304 | tf_op jit(solution)/shard_map/all_to_all | solution.py:14
  67.4 0.0 copy-done
  67.4 0.8 copy.19
  68.3 2.4 %all_to_all.33 = f32[4,128,1024]{2,1,0:T(8,128)} reshape(f32[4,64,2,1024]{3,2,1,0:T(2,128)S(1)} %bitcast.61) | data formatting | bytes 4194304 | tf_op jit(solution)/shard_map/all_to_all | solution.py:14
  70.7 29.1 %all_to_all.42 = f32[4,128,1024]{2,1,0:T(8,128)S(1)} all-to-all(f32[4,128,1024]{2,1,0:T(8,128)} %all_to_all.33), channel_id=1, replica_groups=mesh['rows'=64,'cols'=4] {'cols'}, dimensions={0} | all-to-all | bytes 4194304 | tf_op jit(solution)/shard_map/all_to_all | solution.py:15
  99.8 1.1 multiply_reduce_fusion
  101.6 1.8 fusion.4
  103.4 0.2 fusion.10
  103.6 2.6 %multiply_bitcast_fusion.1 = (f32[1,128,4,1024]{3,1,2,0:T(8,128)}, f32[1,128,4,1024]{3,1,2,0:T(8,128)}) fusion(f32[4,128,1024]{2,1,0:T(8,128)S(1)} %all_to_all.42, f32[]{:T(128)S(6)} %rsqrt.4), kind=kLoop, calls=%fused_computation.14 | loop fusion | flops 1048576 | bytes 6291460 | tf_op jit(solution)/shard_map/mul | solution.py:16
  106.2 1.9 copy.14
  108.1 2.9 %copy.13 = f32[1,128,4,1024]{1,3,2,0:T(8,128)} copy(f32[1,128,4,1024]{3,1,2,0:T(8,128)} %get-tuple-element.7) | data formatting | bytes 4194304 | tf_op jit(solution)/shard_map/mul | solution.py:22
  111.0 2.9 %copy.15 = f32[128,4096]{1,0:T(8,128)} copy(f32[128,4096]{0,1:T(8,128)} %bitcast.62) | data formatting | bytes 4194304 | tf_op jit(solution)/shard_map/mul | solution.py:22
  113.9 3.6 %convolution_add_fusion.3 = f32[128,4096]{1,0:T(8,128)S(1)} fusion(f32[128,4096]{1,0:T(8,128)} %copy.15, f32[128,128]{1,0:T(8,128)S(1)} %fusion.10, f32[128,4096]{0,1:T(8,128)S(1)} %bitcast.60), kind=kOutput, calls=%fused_computation.4 | convolution fusion | flops 805830656 | bytes 6356992 | tf_op jit(solution)/shard_map/mij,mjk->mik/dot_general | solution.py:22
  117.5 1.8 fusion.12
  119.3 0.2 fusion.9
  119.5 2.0 convolution_add_fusion.2
  121.6 1.8 fusion.13
  123.4 0.2 fusion.8
  123.6 2.0 convolution_add_fusion.1
  125.6 1.8 fusion.14
  127.4 0.2 fusion.7
  127.6 2.3 %fusion = f32[1,128,4096]{2,1,0:T(8,128)S(1)} fusion(f32[128,128]{1,0:T(8,128)S(1)} %fusion.7, f32[128,4096]{1,0:T(8,128)S(1)} %convolution_add_fusion.1), kind=kOutput, calls=%fused_computation.1 | convolution fusion | flops 806354944 | bytes 4259840 | tf_op jit(solution)/shard_map/mij,mjk->mik/dot_general | solution.py:22
  129.9 0.2 slice_bitcast_fusion.3
  130.2 0.2 pad_maximum_fusion
  130.4 26.4 %all_to_all.43 = f32[4,1,128,1024]{3,2,1,0:T(8,128)S(1)} all-to-all(f32[4,1,128,1024]{3,2,1,0:T(8,128)S(1)} %pad_maximum_fusion), channel_id=1, replica_groups=mesh['rows'=64,'cols'=4] {'cols'}, dimensions={0} | all-to-all | bytes 4194304 | tf_op jit(solution)/shard_map/all_to_all | solution.py:26
  156.8 1.4 copy.16
  158.2 60.3 %all_to_all.44 = f32[4,128,1024]{2,0,1:T(4,128)S(1)} all-to-all(f32[4,128,1024]{2,0,1:T(4,128)S(1)} %copy.16), channel_id=1, replica_groups=mesh['rows'=64,'cols'=4] {'rows'}, dimensions={1} | all-to-all | bytes 4194304 | tf_op jit(solution)/shard_map/all_to_all | solution.py:29
  218.5 0.6 broadcast_multiply_fusion
  219.1 0.0 copy-start.1
  219.1 1.9 copy.17
  221.0 0.0 copy-done.1
  221.1 2.9 %bitcast_subtract_fusion = f32[256,2,1024]{2,1,0:T(2,128)} fusion(f32[64,4,2,1024]{3,2,1,0:T(2,128)S(1)} %copy.17, f32[256,2,1024]{2,1,0:T(2,128)S(1)} %copy-done.1), kind=kLoop, calls=%fused_computation.8 | loop fusion | flops 1048576 | bytes 6291456 | tf_op jit(solution)/shard_map/sub | solution.py:30
Async XLA Ops:
  4.3 63.2 %copy-start = (f32[256,2,1024]{2,1,0:T(2,128)}, f32[256,2,1024]{2,1,0:T(2,128)S(1)}, u32[]{:S(2)}) copy-start(f32[256,2,1024]{2,1,0:T(2,128)S(1)} %multiply_add_fusion) | copy-start | bytes 6291460
  219.1 2.0 copy-start.1
